TPU v7x, 32 devices: a whole 2x2x4 slice. The times are simulated.
32 devices in a mesh: row: 8 (over y, x, core), col: 4 (over z).
Axes of the slice: x: 2, y: 2, z: 4, core: 2. Of those that a mesh axis runs over, the one named last changes fastest.
Arguments:
- entities: bfloat16 [2, 32768, 200], P(None, ('row', 'col')), may hold values from -2.390625 to 2.390625
- relations: bfloat16 [2, 1024, 200], replicated, may hold values from -6 to 6
- src_index: int32 [131072], P(('row', 'col')), may hold values from 0 to 4095
- dst_index: int32 [131072], P(('row', 'col')), may hold values from 0 to 8191
- rel_index: int32 [131072], P(('row', 'col')), may hold values from 0 to 1023
- neg_block: int32 [256], P(('row', 'col')), may hold values from 0 to 15
Outputs:
- edge_loss: float32 [131072], P(('row', 'col'))
- relation_grad: float32 [2, 1024, 200], P(None, ('row', 'col'))
All inputs are finite; a program needn't handle non-finite values.
Results may differ from a plain program's by a relative error of at most 0.0018.
Values may be sent and summed in bfloat16 or wider, within the bound.
A program may use at most 128 MiB of HBM per device.

v0:
```python
import functools

import jax
import jax.numpy as jnp
from jax import lax
from jax.experimental import pallas as pl
from jax.experimental.pallas import tpu as pltpu
from jax.sharding import PartitionSpec as P

NEGB = 512
LANE = 128
WIDE = 256
MESH = pl.DeviceIdType.MESH
F32 = jnp.float32
BF16 = jnp.bfloat16


def spread_kernel(n_col, ent, src_out, dst_out, loc_sem, send_sem, recv_sem):
    r, c = lax.axis_index("row"), lax.axis_index("col")
    chip, core = r // 2, r % 2
    y, x = chip // 2, chip % 2
    row_of = lambda yy, xx: (yy * 2 + xx) * 2 + core
    xr, yr, dr = row_of(y, 1 - x), row_of(1 - y, x), row_of(1 - y, 1 - x)
    up, down, across = (c + 1) % n_col, (c + n_col - 1) % n_col, (c + 2) % n_col
    mate = (chip * 2 + (1 - core), c)
    above, below, xp, yp = (r, up), (r, down), (xr, c), (yr, c)

    barrier = pltpu.get_barrier_semaphore()
    peers = [mate, above, below, xp, yp]
    for peer in peers:
        pl.semaphore_signal(barrier, inc=1, device_id=peer, device_id_type=MESH)
    pl.semaphore_wait(barrier, len(peers))

    def copy(k, src, dst, peer):
        return pltpu.make_async_remote_copy(
            src_ref=src, dst_ref=dst, send_sem=send_sem.at[k], recv_sem=recv_sem.at[k],
            device_id=peer, device_id_type=MESH,
        )

    own = lambda p: ent.at[p]
    col = lambda i, p: src_out.at[i, p]
    row = lambda i, p: dst_out.at[i, p]
    started = []

    def start(k, src, dst, peer):
        move = copy(k, src, dst, peer)
        move.start()
        started.append(move)

    def arrive(k, dst):
        copy(k, own(0), dst, mate).wait_recv()

    start(0, own(0), col(c, 0), above)
    start(3, own(1), col(c, 1), below)
    start(6, own(0), row(r, 0), xp)
    start(9, own(1), row(r, 1), yp)
    start(1, own(1), col(c, 1), above)
    start(2, own(0), col(c, 0), below)
    start(7, own(1), row(r, 1), xp)
    start(8, own(0), row(r, 0), yp)
    start(12, own(0), row(r, 0), mate)
    start(19, own(1), row(r, 1), mate)
    local = [
        pltpu.make_async_copy(ent, src_out.at[c], loc_sem.at[0]),
        pltpu.make_async_copy(ent, dst_out.at[r], loc_sem.at[1]),
    ]
    for move in local:
        move.start()
    arrive(0, col(down, 0))
    start(4, col(down, 0), col(down, 0), above)
    arrive(3, col(up, 1))
    start(5, col(up, 1), col(up, 1), below)
    arrive(6, row(xr, 0))
    start(10, row(xr, 0), row(xr, 0), yp)
    arrive(9, row(yr, 1))
    start(11, row(yr, 1), row(yr, 1), xp)
    start(13, row(xr, 0), row(xr, 0), mate)
    start(16, row(yr, 1), row(yr, 1), mate)
    arrive(7, row(xr, 1))
    start(14, row(xr, 1), row(xr, 1), mate)
    arrive(8, row(yr, 0))
    start(15, row(yr, 0), row(yr, 0), mate)
    arrive(10, row(dr, 0))
    start(17, row(dr, 0), row(dr, 0), mate)
    arrive(11, row(dr, 1))
    start(18, row(dr, 1), row(dr, 1), mate)
    arrive(1, col(down, 1))
    arrive(2, col(up, 0))
    arrive(4, col(across, 0))
    arrive(5, col(across, 1))
    twin = lambda yy, xx: (yy * 2 + xx) * 2 + (1 - core)
    mx, my, md = twin(y, 1 - x), twin(1 - y, x), twin(1 - y, 1 - x)
    arrive(12, row(mate[0], 0))
    arrive(19, row(mate[0], 1))
    arrive(13, row(mx, 0))
    arrive(14, row(mx, 1))
    arrive(15, row(my, 0))
    arrive(16, row(my, 1))
    arrive(17, row(md, 0))
    arrive(18, row(md, 1))
    for move in started:
        move.wait_send()
    for move in local:
        move.wait()


def spread(n_row, n_col, ent):
    dma = pltpu.SemaphoreType.DMA
    return pl.pallas_call(
        functools.partial(spread_kernel, n_col),
        name="spread",
        out_shape=(
            jax.ShapeDtypeStruct((n_col,) + ent.shape, ent.dtype),
            jax.ShapeDtypeStruct((n_row,) + ent.shape, ent.dtype),
        ),
        in_specs=[pl.BlockSpec(memory_space=pltpu.VMEM)],
        out_specs=(pl.BlockSpec(memory_space=pltpu.HBM), pl.BlockSpec(memory_space=pltpu.HBM)),
        scratch_shapes=[dma((2,)), dma((20,)), dma((20,))],
        compiler_params=pltpu.CompilerParams(collective_id=0, has_side_effects=True),
    )(ent)


def gather_sum_kernel(n_col, acc, out, pair_buf, sa, sb, a1, b1, ta, tb, a2, b2, tot, got, send_sem, recv_sem):
    r, c = lax.axis_index("row"), lax.axis_index("col")
    chip, core = r // 2, r % 2
    y, x = chip // 2, chip % 2
    row_of = lambda yy, xx: (yy * 2 + xx) * 2 + core
    mate = (chip * 2 + (1 - core), c)
    xp, yp = (row_of(y, 1 - x), c), (row_of(1 - y, x), c)
    ring = [(r, (c + b) % n_col) for b in range(1, n_col)]

    barrier = pltpu.get_barrier_semaphore()
    peers = [mate, xp, yp] + ring
    for peer in peers:
        pl.semaphore_signal(barrier, inc=1, device_id=peer, device_id_type=MESH)
    pl.semaphore_wait(barrier, len(peers))

    started = []

    def start(k, src, dst, peer):
        move = pltpu.make_async_remote_copy(
            src_ref=src, dst_ref=dst, send_sem=send_sem.at[k], recv_sem=recv_sem.at[k],
            device_id=peer, device_id_type=MESH,
        )
        move.start()
        started.append(move)
        return move

    spots = [(yy, xx) for yy in range(2) for xx in range(2)]
    pairs = [start(k, acc.at[yy, xx, 1 - core], pair_buf.at[yy, xx], mate) for k, (yy, xx) in enumerate(spots)]
    for move, (yy, xx) in zip(pairs, spots):
        move.wait_recv()
        whole = acc[yy, xx, core] + pair_buf[yy, xx]
        sa[yy, xx] = whole[:, :, :WIDE]
        sb[yy, xx] = whole[:, :, WIDE:]
    move_a = start(4, sa.at[:, 1 - x], a1, xp)
    move_b = start(5, sb.at[1 - y], b1, yp)
    move_a.wait_recv()
    ta[0] = sa[1 - y, x] + a1[1 - y]
    next_a = start(6, ta.at[0], a2, yp)
    ta[1] = sa[y, x] + a1[y]
    move_b.wait_recv()
    tb[0] = sb[y, 1 - x] + b1[1 - x]
    next_b = start(7, tb.at[0], b2, xp)
    tb[1] = sb[y, x] + b1[x]
    next_a.wait_recv()
    tot[:, :, :WIDE] = ta[1] + a2[...]
    next_b.wait_recv()
    tot[:, :, WIDE:] = tb[1] + b2[...]
    hops = [start(8 + b, tot.at[peer[1]], got.at[b], peer) for b, peer in enumerate(ring)]
    total = tot[c]
    for b, move in enumerate(hops):
        move.wait_recv()
        total = total + got[b]
    width = out.shape[2]
    out[0] = total[:, :width]
    out[1] = total[:, WIDE : WIDE + width]
    for move in started:
        move.wait_send()


def gather_sum(n_row, n_col, acc, dim):
    rows = acc.shape[0] // (n_row * n_col)
    wide = acc.shape[1]
    dma = pltpu.SemaphoreType.DMA
    block = lambda *lead: pltpu.VMEM(lead + (n_col, rows, WIDE), F32)
    return pl.pallas_call(
        functools.partial(gather_sum_kernel, n_col),
        name="gather_sum",
        out_shape=jax.ShapeDtypeStruct((2, rows, dim), F32),
        in_specs=[pl.BlockSpec(memory_space=pltpu.VMEM)],
        out_specs=pl.BlockSpec(memory_space=pltpu.VMEM),
        scratch_shapes=[
            pltpu.VMEM((2, 2, n_col, rows, wide), F32),
            block(2, 2), block(2, 2), block(2), block(2), block(2), block(2), block(), block(),
            pltpu.VMEM((n_col, rows, wide), F32),
            pltpu.VMEM((n_col - 1, rows, wide), F32),
            dma((7 + n_col,)), dma((7 + n_col,)),
        ],
        compiler_params=pltpu.CompilerParams(collective_id=1, has_side_effects=True),
    )(acc.reshape(2, 2, 2, n_col, rows, wide))


def edge_kernel(
    group, src_i, dst_i, rel_i, neg_i, rel_row, rel_tab, src_all, dst_all,
    loss, acc, stage, s_tab, o_tab, w_tab, gs, go, gw, neg, qb, pos, term, stage_sem, neg_sem,
):
    n_src, n_dst = src_all.shape[0], dst_all.shape[0]
    ent = src_all.shape[2]
    n_rel = rel_tab.shape[1]
    groups = neg_i.shape[0]
    per = ent // NEGB
    sub = 128

    def neg_copy(g):
        b = neg_i[g]
        return pltpu.make_async_copy(
            dst_all.at[b // per, :, pl.ds(pl.multiple_of((b % per) * NEGB, NEGB), NEGB), :],
            neg.at[g % 2], neg_sem.at[g % 2],
        )

    def fill(table, base, read, rows):
        def step(i, carry):
            row = pl.multiple_of(i * sub, sub)
            for part in range(2):
                for half in range(2):
                    piece = read(part, row, half).astype(F32)
                    table[pl.ds(base + row * 4 + part * 2 + half, sub, stride=4), :] = piece
            return carry

        lax.fori_loop(0, rows // sub, step, 0)

    def load(all_ref, table, count):
        def copy(i):
            return pltpu.make_async_copy(all_ref.at[i], stage.at[i % 2], stage_sem.at[i % 2])

        copy(0).start()

        def step(i, carry):
            @pl.when(i + 1 < count)
            def _():
                copy(i + 1).start()

            copy(i).wait()
            slot = i % 2
            fill(
                table, i * (ent * 4),
                lambda part, row, half: stage[slot, part, pl.ds(row, sub), half * LANE : (half + 1) * LANE], ent,
            )
            return carry

        lax.fori_loop(0, count, step, 0)

    neg_copy(0).start()
    fill(w_tab, 0, lambda part, row, half: rel_tab[part, pl.ds(row, sub), half * LANE : (half + 1) * LANE], n_rel)
    load(src_all, s_tab, n_src)
    load(dst_all, o_tab, n_dst)

    eye = lax.broadcasted_iota(jnp.int32, (sub, LANE), 0) == lax.broadcasted_iota(jnp.int32, (sub, LANE), 1)
    nt = (((1,), (1,)), ((), ()))

    def one_group(g, carry):
        @pl.when(g + 1 < groups)
        def _():
            neg_copy(g + 1).start()

        def pick(i, inner):
            got = []
            for u in range(16):
                e = i * 16 + u
                a = pl.multiple_of(src_i[g * group + e] * 4, 4)
                b = pl.multiple_of(dst_i[g * group + e] * 4, 4)
                k = pl.multiple_of(rel_i[g * group + e] * 4, 4)
                got.append((s_tab[pl.ds(a, 4), :], o_tab[pl.ds(b, 4), :], w_tab[pl.ds(k, 4), :]))
            for u in range(16):
                at = pl.ds(pl.multiple_of((i * 16 + u) * 4, 4), 4)
                gs[at, :], go[at, :], gw[at, :] = got[u]
            return inner

        lax.fori_loop(0, group // 16, pick, 0)

        qrows = 32

        def query(i, inner):
            row = pl.multiple_of(i * qrows, qrows)
            score = None
            for half in range(2):
                part = lambda ref, p: ref[pl.ds(row * 4 + p * 2 + half, qrows, stride=4), :]
                sr, si, wr, wi = part(gs, 0), part(gs, 1), part(gw, 0), part(gw, 1)
                qr = sr * wr - si * wi
                qi = sr * wi + si * wr
                add = qr * part(go, 0) + qi * part(go, 1)
                score = add if score is None else score + add
                qb[pl.ds(row, qrows), half * LANE : (half + 1) * LANE] = qr.astype(BF16)
                qb[pl.ds(row, qrows), WIDE + half * LANE : WIDE + (half + 1) * LANE] = qi.astype(BF16)
            pos[pl.ds(row, qrows), :] = jnp.sum(score, 1, keepdims=True)
            return inner

        lax.fori_loop(0, group // qrows, query, 0)
        neg_copy(g).wait()
        slot = g % 2

        def block(i, inner):
            row = pl.multiple_of(i * sub, sub)
            rows = pl.ds(row, sub)
            n_re, n_im = neg[slot, 0], neg[slot, 1]
            score = lax.dot_general(qb[rows, :WIDE], n_re, nt, preferred_element_type=F32)
            score = score + lax.dot_general(qb[rows, WIDE:], n_im, nt, preferred_element_type=F32)
            small = jnp.exp(-jnp.abs(score))
            soft = jnp.maximum(score, 0.0) + jnp.log1p(small)
            weight = (jnp.where(score >= 0.0, 1.0, small) / (1.0 + small) * (1.0 / NEGB)).astype(BF16)
            p = pos[rows, :]
            p_small = jnp.exp(-jnp.abs(p))
            value = jnp.maximum(-p, 0.0) + jnp.log1p(p_small) + jnp.sum(soft, 1, keepdims=True) * (1.0 / NEGB)
            pull = jnp.where(p >= 0.0, p_small, 1.0) / (1.0 + p_small)
            loss[pl.ds(g * (group // sub) + i, 1), :] = jnp.sum(jnp.where(eye, value, 0.0), 0, keepdims=True)
            g_re = jnp.dot(weight, n_re, preferred_element_type=F32)
            g_im = jnp.dot(weight, n_im, preferred_element_type=F32)
            for half in range(2):
                part = lambda ref, q: ref[pl.ds(row * 4 + q * 2 + half, sub, stride=4), :]
                cols = slice(half * LANE, (half + 1) * LANE)
                d_re = g_re[:, cols] - pull * part(go, 0)
                d_im = g_im[:, cols] - pull * part(go, 1)
                s_re, s_im = part(gs, 0), part(gs, 1)
                at = pl.ds(pl.multiple_of(g * group + row, sub), sub)
                term[at, half * LANE : (half + 1) * LANE] = (d_re * s_re + d_im * s_im).astype(BF16)
                term[at, WIDE + half * LANE : WIDE + (half + 1) * LANE] = (d_im * s_re - d_re * s_im).astype(BF16)
            return inner

        lax.fori_loop(0, group // sub, block, 0)
        return carry

    lax.fori_loop(0, groups, one_group, 0)

    tile = 256
    edges = term.shape[0]

    def reduce(i, carry):
        row = pl.multiple_of(i * tile, tile)
        ids = lax.broadcasted_iota(jnp.int32, (tile, edges), 0) + row
        hot = jnp.where(ids == rel_row[...], 1.0, 0.0).astype(BF16)
        acc[pl.ds(row, tile), :] = jnp.dot(hot, term[...], preferred_element_type=F32)
        return carry

    lax.fori_loop(0, n_rel // tile, reduce, 0)


def edge_terms(src_all, dst_all, relations, src_index, dst_index, rel_index, neg_block):
    edges, groups = src_index.shape[0], neg_block.shape[0]
    group = edges // groups
    n_rel = relations.shape[1]
    ent = src_all.shape[2]
    smem = pl.BlockSpec(memory_space=pltpu.SMEM)
    vmem = pl.BlockSpec(memory_space=pltpu.VMEM)
    hbm = pl.BlockSpec(memory_space=pltpu.HBM)
    quad = 4
    return pl.pallas_call(
        functools.partial(edge_kernel, group),
        name="edge_terms",
        out_shape=(
            jax.ShapeDtypeStruct((edges // LANE, LANE), F32),
            jax.ShapeDtypeStruct((n_rel, 2 * WIDE), F32),
        ),
        in_specs=[smem, smem, smem, smem, vmem, vmem, hbm, hbm],
        out_specs=(vmem, vmem),
        scratch_shapes=[
            pltpu.VMEM((2, 2, ent, WIDE), BF16),
            pltpu.VMEM((src_all.shape[0] * ent * quad, LANE), F32),
            pltpu.VMEM((dst_all.shape[0] * ent * quad, LANE), F32),
            pltpu.VMEM((n_rel * quad, LANE), F32),
            pltpu.VMEM((group * quad, LANE), F32),
            pltpu.VMEM((group * quad, LANE), F32),
            pltpu.VMEM((group * quad, LANE), F32),
            pltpu.VMEM((2, 2, NEGB, WIDE), BF16),
            pltpu.VMEM((group, 2 * WIDE), BF16),
            pltpu.VMEM((group, 1), F32),
            pltpu.VMEM((edges, 2 * WIDE), BF16),
            pltpu.SemaphoreType.DMA((2,)),
            pltpu.SemaphoreType.DMA((2,)),
        ],
        compiler_params=pltpu.CompilerParams(vmem_limit_bytes=62 * 2**20),
    )(
        src_index, dst_index, rel_index, neg_block, rel_index.reshape(1, edges), relations, src_all, dst_all,
    )


def body(n_row, n_col, entities, relations, src_index, dst_index, rel_index, neg_block):
    dim = entities.shape[2]
    ent = entities.shape[1]
    pad = ((0, 0), (0, 0), (0, WIDE - dim))
    if n_row != 8 or n_col != 4 or (n_row + n_col) * ent * 4 * LANE * 4 > 36 * 2**20:
        return wide_body(entities, relations, src_index, dst_index, rel_index, neg_block)
    src_all, dst_all = spread(n_row, n_col, jnp.pad(entities, pad))
    edge_loss, acc = edge_terms(
        src_all, dst_all, jnp.pad(relations, pad), src_index, dst_index, rel_index, neg_block
    )
    grad = gather_sum(n_row, n_col, acc, dim)
    return edge_loss.reshape(-1), grad


def bucket_terms(picked_src, picked_dst, negatives, relations, rel_ids):
    onehot = (rel_ids[:, None] == jnp.arange(relations.shape[1], dtype=jnp.int32)[None, :]).astype(
        jnp.bfloat16
    )
    rel_re = jnp.dot(onehot, relations[0], preferred_element_type=jnp.float32)
    rel_im = jnp.dot(onehot, relations[1], preferred_element_type=jnp.float32)
    src_re = picked_src[0].astype(jnp.float32)
    src_im = picked_src[1].astype(jnp.float32)
    dst_re = picked_dst[0].astype(jnp.float32)
    dst_im = picked_dst[1].astype(jnp.float32)
    query_re = src_re * rel_re - src_im * rel_im
    query_im = src_re * rel_im + src_im * rel_re
    pos_score = jnp.sum(query_re * dst_re, 1) + jnp.sum(query_im * dst_im, 1)
    groups = negatives.shape[1]
    dim = query_re.shape[1]
    qre_b = query_re.astype(jnp.bfloat16).reshape(groups, -1, dim)
    qim_b = query_im.astype(jnp.bfloat16).reshape(groups, -1, dim)
    neg_score = jnp.einsum(
        "kcd,knd->kcn", qre_b, negatives[0], preferred_element_type=jnp.float32
    ) + jnp.einsum("kcd,knd->kcn", qim_b, negatives[1], preferred_element_type=jnp.float32)
    edge_loss = jax.nn.softplus(-pos_score) + jnp.mean(jax.nn.softplus(neg_score), -1).reshape(-1)
    weights = (jax.nn.sigmoid(neg_score) / NEGB).astype(jnp.bfloat16)
    gneg_re = jnp.einsum(
        "kcn,knd->kcd", weights, negatives[0], preferred_element_type=jnp.float32
    ).reshape(-1, dim)
    gneg_im = jnp.einsum(
        "kcn,knd->kcd", weights, negatives[1], preferred_element_type=jnp.float32
    ).reshape(-1, dim)
    pull = jax.nn.sigmoid(-pos_score)[:, None]
    grad_re = gneg_re - pull * dst_re
    grad_im = gneg_im - pull * dst_im
    term_re = (grad_re * src_re + grad_im * src_im).astype(jnp.bfloat16)
    term_im = (grad_im * src_re - grad_re * src_im).astype(jnp.bfloat16)
    dims = (((0,), (0,)), ((), ()))
    rel_grad = jnp.stack(
        [
            lax.dot_general(onehot, term_re, dims, preferred_element_type=jnp.float32),
            lax.dot_general(onehot, term_im, dims, preferred_element_type=jnp.float32),
        ],
        0,
    )
    return (edge_loss, rel_grad)


def wide_body(entities, relations, src_index, dst_index, rel_index, neg_block):
    dim = entities.shape[2]
    source_rows = lax.all_gather(entities, "col", axis=1, tiled=True)
    picked_src = jnp.take(source_rows, src_index, axis=1)
    target_rows = lax.all_gather(entities, "row", axis=1, tiled=True)
    picked_dst = jnp.take(target_rows, dst_index, axis=1)
    negatives = jnp.take(target_rows.reshape(2, -1, NEGB, dim), neg_block, axis=1)
    edge_loss, rel_grad = bucket_terms(picked_src, picked_dst, negatives, relations, rel_index)
    row_share = lax.psum_scatter(rel_grad, "row", scatter_dimension=1, tiled=True)
    grad_share = lax.psum_scatter(row_share, "col", scatter_dimension=1, tiled=True)
    return (edge_loss, grad_share)


def solution(mesh):
    placed = (
        P(None, ("row", "col"), None),
        P(),
        P(("row", "col")),
        P(("row", "col")),
        P(("row", "col")),
        P(("row", "col")),
    )
    return jax.shard_map(
        functools.partial(body, mesh.shape["row"], mesh.shape["col"]),
        mesh=mesh,
        in_specs=placed,
        out_specs=(P(("row", "col")), P(None, ("row", "col"), None)),
        check_vma=False,
    )
```

profile of v0, /device:TPU:0, one launch (start us, length us, event | category | flops | bytes accessed | tf_op | source)
XLA Modules:
  0.0 173.5 jit_solution(5333554919482069002)
XLA Ops:
  0.6 0.0 copy-start
  0.6 1.5 copy.9
  2.2 1.2 pad.8.ent
  3.4 0.0 copy-done
  3.4 0.5 copy.8
  3.9 1.2 pad.7.rel_tab
  5.1 74.2 %spread.1 = (bf16[4,2,1024,256]{3,2,1,0:T(8,128)(2,1)}, bf16[8,2,1024,256]{3,2,1,0:T(8,128)(2,1)}) custom-call(bf16[2,1024,256]{2,1,0:T(8,128)(2,1)} %pad.8.ent), custom_call_target="tpu_custom_call" | custom-call | tf_op jit(solution)/shard_map/spread/pallas_call | solution.py:109
  79.3 65.6 %edge_terms.1 = (f32[32,128]{1,0:T(8,128)}, f32[1024,512]{1,0:T(8,128)}) custom-call(s32[4096]{0:T(1024)} %src_i.1, s32[4096]{0:T(1024)} %dst_i.1, s32[4096]{0:T(1024)} %rel_i.1, s32[8]{0:T(128)} %neg_i.1, s32[1,4096]{1,0:T(1,128)} %bitcast.4, bf16[2,1024,256]{2,1,0:T(8,128)(2,1)} %pad.7.rel_tab, bf16[4,2,1024,256]{3,2,1,0:T(8,128)(2,1)} %get-tuple-element.6.src_all, ...), custom_call_target="tpu_custom_call" | custom-call | tf_op jit(solution)/shard_map/edge_terms/pallas_call | solution.py:357
  144.9 27.1 %gather_sum.1 = f32[2,32,200]{2,1,0:T(8,128)} custom-call(f32[2,2,2,4,32,512]{5,4,3,2,1,0:T(8,128)} %bitcast.3), custom_call_target="tpu_custom_call" | custom-call | tf_op jit(solution)/shard_map/gather_sum/pallas_call | solution.py:187
  172.1 1.5 copy.11
Async XLA Ops:
  0.6 2.7 %copy-start = (bf16[2,1024,200]{1,2,0:T(8,128)(2,1)S(1)}, bf16[2,1024,200]{1,2,0:T(8,128)(2,1)}, u32[]{:S(2)}) copy-start(bf16[2,1024,200]{1,2,0:T(8,128)(2,1)} %param.7) | copy-start | bytes 2457604
where the time goes:
time: 174 us
  Pallas kernels  167 us (96%)
  local copies, waits for them, and re-layouts  5.89 us (3%)
    pallas_call x1, Pallas kernels, spread(): pl.pallas_call(functools.partial(spread_kernel, n_col), name='spread', ou...  74.2 us
    pallas_call x1, Pallas kernels, edge_terms(): pl.pallas_call(functools.partial(edge_kernel, group), name='edge_terms',...  65.6 us
    pallas_call x1, Pallas kernels, gather_sum(): pl.pallas_call(functools.partial(gather_sum_kernel, n_col), name='gather_...  27.1 us
    unnamed x5, local copies, waits for them, and re-layouts  3.5 us

commit v1 on v0

v1 whole, which is shorter than its diff:
```python
import functools

import jax
import jax.numpy as jnp
from jax import lax
from jax.experimental import pallas as pl
from jax.experimental.pallas import tpu as pltpu
from jax.sharding import PartitionSpec as P

NEGB = 512
LANE = 128
WIDE = 256
MESH = pl.DeviceIdType.MESH
F32 = jnp.float32
BF16 = jnp.bfloat16
PICKS = 32
QROWS = 32


def log1p_small(u):
    return jnp.where(u < 2.0**-9, u - 0.5 * u * u, jnp.log(1.0 + u))


def step_kernel(
    n_col, group, src_i, dst_i, rel_i, neg_i, rel_row, ent, rel, loss, grad,
    srcb, dstb, relb, s_tab, o_tab, w_tab, gs, go, gw, qb, pos, key, acc, pairb, tot, inb, zs, zin,
    loc_sem, send_sem, recv_sem,
):
    r, c = lax.axis_index("row"), lax.axis_index("col")
    chip, core = r // 2, r % 2
    y, x = chip // 2, chip % 2
    row_of = lambda yy, xx, k: (yy * 2 + xx) * 2 + k
    xr, yr, dr = row_of(y, 1 - x, core), row_of(1 - y, x, core), row_of(1 - y, 1 - x, core)
    mr, mx, my, md = (row_of(yy, xx, 1 - core) for yy, xx in ((y, x), (y, 1 - x), (1 - y, x), (1 - y, 1 - x)))
    mate, xp, yp, dp = (mr, c), (xr, c), (yr, c), (dr, c)
    dim, count = ent.shape[1], ent.shape[2]
    n_rel = rel.shape[2]
    groups = neg_i.shape[0]
    per = count // NEGB
    rest = dim - LANE

    barrier = pltpu.get_barrier_semaphore()
    peers = [mate, xp, yp, dp] + [(r, (c + b) % n_col) for b in range(1, n_col)]
    for peer in peers:
        pl.semaphore_signal(barrier, inc=1, device_id=peer, device_id_type=MESH)
    pl.semaphore_wait(barrier, len(peers))

    started = []

    def copy(k, src, dst, peer):
        return pltpu.make_async_remote_copy(
            src_ref=src, dst_ref=dst, send_sem=send_sem.at[k], recv_sem=recv_sem.at[k],
            device_id=peer, device_id_type=MESH,
        )

    def start(k, src, dst, peer):
        move = copy(k, src, dst, peer)
        move.start()
        started.append((None, move))

    def arrive(k, dst):
        copy(k, dst, dst, mate).wait_recv()

    own = lambda p: ent.at[:, :, p * NEGB : (p + 1) * NEGB]
    inside = lambda v: jnp.logical_and(v >= 0, v < n_col)

    def line_id(way, age, part):
        return ((0 if way > 0 else n_col - 1) + age) * 2 + part

    def line_send(way, age, part):
        shard = c - way * age
        cond = jnp.logical_and(inside(c + way), inside(shard))
        src = own(part) if age == 0 else srcb.at[shard * per + part]
        move = copy(line_id(way, age, part), src, srcb.at[shard * per + part], (r, c + way))

        @pl.when(cond)
        def _():
            move.start()

        started.append((cond, move))

    def line_wait(way, age, part):
        shard = c - way * (age + 1)

        @pl.when(inside(shard))
        def _():
            arrive(line_id(way, age, part), srcb.at[shard * per + part])

    base = 4 * (n_col - 1)
    X0, X1, Y0, Y1, XD, YD, M0 = (base + k for k in range(7))
    at_dst = lambda i, p: dstb.at[i * per + p]

    line_send(1, 0, 0)
    line_send(-1, 0, 0)
    start(X0, own(0), at_dst(r, 0), xp)
    start(Y1, own(1), at_dst(r, 1), yp)
    local_rel = pltpu.make_async_copy(rel, relb, loc_sem.at[0])
    local_ent = [pltpu.make_async_copy(own(p), at_dst(r, p), loc_sem.at[1 + p]) for p in range(per)]
    local_rel.start()
    for move in local_ent:
        move.start()
    line_send(1, 0, 1)
    line_send(-1, 0, 1)
    start(X1, own(1), at_dst(r, 1), xp)
    start(Y0, own(0), at_dst(r, 0), yp)
    start(M0, own(0), at_dst(r, 0), mate)
    start(M0 + 1, own(1), at_dst(r, 1), mate)

    def fill(read, targets):
        def step(j, carry):
            col = pl.multiple_of(j * LANE, LANE)
            for part in range(2):
                low = read(part, slice(0, LANE), col).astype(F32).T
                high = read(part, slice(LANE, dim), col).astype(F32)
                high = jnp.concatenate([high, jnp.zeros((LANE - rest, LANE), F32)], 0).T
                for table, first, _ in targets:
                    flat = table.reshape(table.shape[0] * 4, LANE)
                    at = first + col * 4 + part * 2
                    flat[pl.ds(at, LANE, stride=4), :] = low
                    flat[pl.ds(at + 1, LANE, stride=4), :] = high
            return carry

        lax.fori_loop(0, targets[0][2] // LANE, step, 0)

    def fill_half(buf, half, *tables):
        fill(
            lambda p, rows, col: buf[half, p, rows, pl.ds(col, LANE)],
            [(table, shard * (NEGB * 4), NEGB) for table, shard in tables],
        )

    def fill_dst(shard):
        for p in range(per):
            half = shard * per + p
            fill_half(dstb, half, (o_tab, half))

    def fill_src(shard):
        @pl.when(inside(shard))
        def _():
            for p in range(per):
                half = shard * per + p
                fill_half(srcb, half, (s_tab, half))

    def pick(table, index, g):
        def step(i, carry):
            got = []
            for u in range(PICKS):
                got.append(table[index[g * group + i * PICKS + u]])
            for u in range(PICKS):
                gs[pl.ds(pl.multiple_of((i * PICKS + u) * 4, 4), 4), :] = got[u]
            return carry

        lax.fori_loop(0, group // PICKS, step, 0)

    def pick_all(table, index, out):
        def one(g, carry):
            pick(table, index, g)

            def pack(i, inner):
                row = pl.multiple_of(i * QROWS, QROWS)
                at = pl.ds(pl.multiple_of(g * group + row, QROWS), QROWS)
                for k in range(4):
                    out[at, k * LANE : (k + 1) * LANE] = gs[pl.ds(row * 4 + k, QROWS, stride=4), :].astype(BF16)
                return inner

            lax.fori_loop(0, group // QROWS, pack, 0)
            return carry

        lax.fori_loop(0, groups, one, 0)

    rel_ids = rel_row[...]
    span = n_rel // (8 * n_col)
    row_part = lax.div(rel_ids, n_col * span)
    key[...] = (
        lax.rem(lax.div(rel_ids, span), n_col) * (8 * span)
        + lax.rem(row_part, 2) * (4 * span) + lax.div(row_part, 2) * span + lax.rem(rel_ids, span)
    )

    local_rel.wait()
    fill(lambda p, rows, col: relb[p, rows, pl.ds(col, LANE)], [(w_tab, 0, n_rel)])
    pick_all(w_tab, rel_i, gw)
    for move in local_ent:
        move.wait()
    for p in range(per):
        fill_half(dstb, r * per + p, (o_tab, r * per + p), (s_tab, c * per + p))

    arrive(X0, at_dst(xr, 0))
    start(YD, at_dst(xr, 0), at_dst(xr, 0), yp)
    arrive(Y1, at_dst(yr, 1))
    start(XD, at_dst(yr, 1), at_dst(yr, 1), xp)
    for way in (1, -1):
        line_wait(way, 0, 0)
        line_send(way, 1, 0)
    start(M0 + 2, at_dst(xr, 0), at_dst(xr, 0), mate)
    start(M0 + 3, at_dst(yr, 1), at_dst(yr, 1), mate)
    arrive(M0, at_dst(mr, 0))
    arrive(M0 + 1, at_dst(mr, 1))
    fill_dst(mr)

    arrive(X1, at_dst(xr, 1))
    start(M0 + 4, at_dst(xr, 1), at_dst(xr, 1), mate)
    arrive(Y0, at_dst(yr, 0))
    start(M0 + 5, at_dst(yr, 0), at_dst(yr, 0), mate)
    for way in (1, -1):
        line_wait(way, 0, 1)
        line_send(way, 1, 1)
    fill_dst(xr)
    fill_dst(yr)
    fill_src(c - 1)
    fill_src(c + 1)
    arrive(M0 + 2, at_dst(mx, 0))
    arrive(M0 + 4, at_dst(mx, 1))
    fill_dst(mx)
    arrive(M0 + 3, at_dst(my, 1))
    arrive(M0 + 5, at_dst(my, 0))
    fill_dst(my)

    arrive(YD, at_dst(dr, 0))
    start(M0 + 6, at_dst(dr, 0), at_dst(dr, 0), mate)
    arrive(XD, at_dst(dr, 1))
    start(M0 + 7, at_dst(dr, 1), at_dst(dr, 1), mate)
    for way in (1, -1):
        line_wait(way, 1, 0)
        line_send(way, 2, 0)
    fill_dst(dr)
    arrive(M0 + 6, at_dst(md, 0))
    arrive(M0 + 7, at_dst(md, 1))
    fill_dst(md)
    pick_all(o_tab, dst_i, go)

    for way in (1, -1):
        line_wait(way, 1, 1)
        line_send(way, 2, 1)
    fill_src(c - 2)
    fill_src(c + 2)
    for way in (1, -1):
        line_wait(way, 2, 0)
        line_wait(way, 2, 1)
    fill_src(c - 3)
    fill_src(c + 3)

    eye = lax.broadcasted_iota(jnp.int32, (LANE, LANE), 0) == lax.broadcasted_iota(jnp.int32, (LANE, LANE), 1)
    nt = (((1,), (1,)), ((), ()))
    cuts = ((0, LANE), (LANE, dim))

    def one_group(g, carry):
        pick(s_tab, src_i, g)

        def query(i, inner):
            row = pl.multiple_of(i * QROWS, QROWS)
            rows = pl.ds(pl.multiple_of(g * group + row, QROWS), QROWS)
            score = None
            for half, (low, high) in enumerate(cuts):
                near = lambda p: gs[pl.ds(row * 4 + p * 2 + half, QROWS, stride=4), :]
                dense = lambda ref, p: ref[rows, p * WIDE + half * LANE : p * WIDE + (half + 1) * LANE].astype(F32)
                sr, si, wr, wi = near(0), near(1), dense(gw, 0), dense(gw, 1)
                qr = sr * wr - si * wi
                qi = sr * wi + si * wr
                add = qr * dense(go, 0) + qi * dense(go, 1)
                score = add if score is None else score + add
                qb[0, pl.ds(row, QROWS), low:high] = qr[:, : high - low].astype(BF16)
                qb[1, pl.ds(row, QROWS), low:high] = qi[:, : high - low].astype(BF16)
            pos[pl.ds(row, QROWS), :] = jnp.sum(score, 1, keepdims=True)
            return inner

        lax.fori_loop(0, group // QROWS, query, 0)

        b = neg_i[g]
        near = lambda p: dstb[b, p]
        score = jnp.dot(qb[0], near(0), preferred_element_type=F32)
        score = score + jnp.dot(qb[1], near(1), preferred_element_type=F32)
        small = jnp.exp(-jnp.abs(score))
        soft = jnp.maximum(score, 0.0) + log1p_small(small)
        turn = 1.0 / (1.0 + small)
        weight = jnp.where(score >= 0.0, turn, small * turn).astype(BF16)
        p = pos[...]
        p_small = jnp.exp(-jnp.abs(p))
        value = jnp.maximum(-p, 0.0) + log1p_small(p_small) + jnp.sum(soft, 1, keepdims=True) * (1.0 / NEGB)
        pull = jnp.where(p >= 0.0, p_small, 1.0) / (1.0 + p_small)
        for i in range(group // LANE):
            piece = value[i * LANE : (i + 1) * LANE]
            loss[pl.ds(g * (group // LANE) + i, 1), :] = jnp.sum(jnp.where(eye, piece, 0.0), 0, keepdims=True)
        g_re = lax.dot_general(weight, near(0), nt, preferred_element_type=F32) * (1.0 / NEGB)
        g_im = lax.dot_general(weight, near(1), nt, preferred_element_type=F32) * (1.0 / NEGB)
        rows = pl.ds(pl.multiple_of(g * group, group), group)
        for half, (low, high) in enumerate(cuts):
            wide = high - low
            part = lambda q: gs[pl.ds(q * 2 + half, group, stride=4), :][:, :wide]
            lanes = lambda q: slice(q * WIDE + low, q * WIDE + high)
            d_re = g_re[:, low:high] - pull * go[rows, lanes(0)].astype(F32)
            d_im = g_im[:, low:high] - pull * go[rows, lanes(1)].astype(F32)
            s_re, s_im = part(0), part(1)
            gw[rows, lanes(0)] = (d_re * s_re + d_im * s_im).astype(BF16)
            gw[rows, lanes(1)] = (d_im * s_re - d_re * s_im).astype(BF16)
        return carry

    lax.fori_loop(0, groups, one_group, 0)

    tile = 8 * span
    edges = gw.shape[0]
    home = [2, 1, 3, 0]
    S0 = M0 + 8
    spots = [(xp, (y * 2 + 1 - x)), (yp, ((1 - y) * 2 + x)), (dp, ((1 - y) * 2 + 1 - x))]
    order = [2, 0, 1]

    def pair_up(t):
        arrive(S0 + t, pairb.at[t])
        tot[t] = acc[t, core] + pairb[t]
        for k in order:
            peer, there = spots[k]
            start(S0 + 4 + t * 3 + k, tot.at[t, there], inb.at[t, k], peer)

    def plane_sum(t):
        total = tot[t, chip]
        for k in range(3):
            arrive(S0 + 4 + t * 3 + k, inb.at[t, k])
            total = total + inb[t, k]
        return total

    for t in range(n_col):
        plane = (c + home[t]) % n_col
        ids = lax.broadcasted_iota(jnp.int32, (tile, edges), 0) + plane * tile
        hot = jnp.where(ids == key[...], 1.0, 0.0).astype(BF16)
        acc[t] = jnp.dot(hot, gw[...], preferred_element_type=F32).reshape(2, 4, span, 2 * WIDE)
        start(S0 + t, acc.at[t, 1 - core], pairb.at[t], mate)
        if t:
            pair_up(t - 1)
    pair_up(n_col - 1)
    Z0 = S0 + 4 + n_col * 3
    for t in range(n_col - 1):
        zs[t] = plane_sum(t)
        start(Z0 + t, zs.at[t], zin.at[t], (r, (c + home[t]) % n_col))
    total = plane_sum(n_col - 1)
    for t in range(n_col - 1):
        arrive(Z0 + t, zin.at[t])
        total = total + zin[t]
    grad[0] = total[:, :dim]
    grad[1] = total[:, WIDE : WIDE + dim]

    for cond, move in started:
        if cond is None:
            move.wait_send()
        else:
            pl.when(cond)(move.wait_send)


def step_call(n_row, n_col, ent, rel, src_index, dst_index, rel_index, neg_block):
    edges, groups = src_index.shape[0], neg_block.shape[0]
    group = edges // groups
    parts, dim, count = ent.shape
    n_rel = rel.shape[2]
    span = n_rel // (n_row * n_col)
    chips = n_row // 2
    smem = pl.BlockSpec(memory_space=pltpu.SMEM)
    vmem = pl.BlockSpec(memory_space=pltpu.VMEM)
    hbm = pl.BlockSpec(memory_space=pltpu.HBM)
    dma = pltpu.SemaphoreType.DMA
    copies = 4 * (n_col - 1) + 14 + 4 + n_col * 3 + n_col - 1
    return pl.pallas_call(
        functools.partial(step_kernel, n_col, group),
        name="step",
        out_shape=(
            jax.ShapeDtypeStruct((edges // LANE, LANE), F32),
            jax.ShapeDtypeStruct((parts, span, dim), F32),
        ),
        in_specs=[smem, smem, smem, smem, vmem, hbm, hbm],
        out_specs=(vmem, vmem),
        scratch_shapes=[
            pltpu.VMEM((n_col * count // NEGB, parts, dim, NEGB), BF16),
            pltpu.VMEM((n_row * count // NEGB, parts, dim, NEGB), BF16),
            pltpu.VMEM(rel.shape, BF16),
            pltpu.VMEM((n_col * count, 4, LANE), F32),
            pltpu.VMEM((n_row * count, 4, LANE), F32),
            pltpu.VMEM((n_rel, 4, LANE), F32),
            pltpu.VMEM((group * 4, LANE), F32),
            pltpu.VMEM((edges, 2 * WIDE), BF16),
            pltpu.VMEM((edges, 2 * WIDE), BF16),
            pltpu.VMEM((parts, group, dim), BF16),
            pltpu.VMEM((group, 1), F32),
            pltpu.VMEM((1, edges), jnp.int32),
            pltpu.VMEM((n_col, 2, chips, span, 2 * WIDE), F32),
            pltpu.VMEM((n_col, chips, span, 2 * WIDE), F32),
            pltpu.VMEM((n_col, chips, span, 2 * WIDE), F32),
            pltpu.VMEM((n_col, 3, span, 2 * WIDE), F32),
            pltpu.VMEM((n_col - 1, span, 2 * WIDE), F32),
            pltpu.VMEM((n_col - 1, span, 2 * WIDE), F32),
            dma((3,)), dma((copies,)), dma((copies,)),
        ],
        compiler_params=pltpu.CompilerParams(
            collective_id=0, has_side_effects=True, vmem_limit_bytes=67043328
        ),
    )(src_index, dst_index, rel_index, neg_block, rel_index.reshape(1, edges), ent, rel)


def body(n_row, n_col, entities, relations, src_index, dst_index, rel_index, neg_block):
    dim = entities.shape[2]
    count = entities.shape[1]
    args = (entities, relations, src_index, dst_index, rel_index, neg_block)
    fits = LANE < dim < WIDE and (n_row + n_col) * count * 4 * LANE * 4 <= 26 * 2**20
    if n_row != 8 or n_col != 4 or count != 2 * NEGB or not fits:
        return wide_body(*args)
    flip = lambda a: jnp.transpose(a, (0, 2, 1))
    edge_loss, grad = step_call(
        n_row, n_col, flip(entities), flip(relations), src_index, dst_index, rel_index, neg_block
    )
    return edge_loss.reshape(-1), grad


def bucket_terms(picked_src, picked_dst, negatives, relations, rel_ids):
    onehot = (rel_ids[:, None] == jnp.arange(relations.shape[1], dtype=jnp.int32)[None, :]).astype(
        jnp.bfloat16
    )
    rel_re = jnp.dot(onehot, relations[0], preferred_element_type=jnp.float32)
    rel_im = jnp.dot(onehot, relations[1], preferred_element_type=jnp.float32)
    src_re = picked_src[0].astype(jnp.float32)
    src_im = picked_src[1].astype(jnp.float32)
    dst_re = picked_dst[0].astype(jnp.float32)
    dst_im = picked_dst[1].astype(jnp.float32)
    query_re = src_re * rel_re - src_im * rel_im
    query_im = src_re * rel_im + src_im * rel_re
    pos_score = jnp.sum(query_re * dst_re, 1) + jnp.sum(query_im * dst_im, 1)
    groups = negatives.shape[1]
    dim = query_re.shape[1]
    qre_b = query_re.astype(jnp.bfloat16).reshape(groups, -1, dim)
    qim_b = query_im.astype(jnp.bfloat16).reshape(groups, -1, dim)
    neg_score = jnp.einsum(
        "kcd,knd->kcn", qre_b, negatives[0], preferred_element_type=jnp.float32
    ) + jnp.einsum("kcd,knd->kcn", qim_b, negatives[1], preferred_element_type=jnp.float32)
    edge_loss = jax.nn.softplus(-pos_score) + jnp.mean(jax.nn.softplus(neg_score), -1).reshape(-1)
    weights = (jax.nn.sigmoid(neg_score) / NEGB).astype(jnp.bfloat16)
    gneg_re = jnp.einsum(
        "kcn,knd->kcd", weights, negatives[0], preferred_element_type=jnp.float32
    ).reshape(-1, dim)
    gneg_im = jnp.einsum(
        "kcn,knd->kcd", weights, negatives[1], preferred_element_type=jnp.float32
    ).reshape(-1, dim)
    pull = jax.nn.sigmoid(-pos_score)[:, None]
    grad_re = gneg_re - pull * dst_re
    grad_im = gneg_im - pull * dst_im
    term_re = (grad_re * src_re + grad_im * src_im).astype(jnp.bfloat16)
    term_im = (grad_im * src_re - grad_re * src_im).astype(jnp.bfloat16)
    dims = (((0,), (0,)), ((), ()))
    rel_grad = jnp.stack(
        [
            lax.dot_general(onehot, term_re, dims, preferred_element_type=jnp.float32),
            lax.dot_general(onehot, term_im, dims, preferred_element_type=jnp.float32),
        ],
        0,
    )
    return (edge_loss, rel_grad)


def wide_body(entities, relations, src_index, dst_index, rel_index, neg_block):
    dim = entities.shape[2]
    source_rows = lax.all_gather(entities, "col", axis=1, tiled=True)
    picked_src = jnp.take(source_rows, src_index, axis=1)
    target_rows = lax.all_gather(entities, "row", axis=1, tiled=True)
    picked_dst = jnp.take(target_rows, dst_index, axis=1)
    negatives = jnp.take(target_rows.reshape(2, -1, NEGB, dim), neg_block, axis=1)
    edge_loss, rel_grad = bucket_terms(picked_src, picked_dst, negatives, relations, rel_index)
    row_share = lax.psum_scatter(rel_grad, "row", scatter_dimension=1, tiled=True)
    grad_share = lax.psum_scatter(row_share, "col", scatter_dimension=1, tiled=True)
    return (edge_loss, grad_share)


def solution(mesh):
    placed = (
        P(None, ("row", "col"), None),
        P(),
        P(("row", "col")),
        P(("row", "col")),
        P(("row", "col")),
        P(("row", "col")),
    )
    return jax.shard_map(
        functools.partial(body, mesh.shape["row"], mesh.shape["col"]),
        mesh=mesh,
        in_specs=placed,
        out_specs=(P(("row", "col")), P(None, ("row", "col"), None)),
        check_vma=False,
    )
```

time: 174 us -> 113 us (0.65)
  Pallas kernels: 167 us -> 109 us
  local copies, waits for them, and re-layouts: 5.89 us -> 2.8 us
    pallas_call x3 -> x1, Pallas kernels: 167 us -> 109 us  [step_call(): pl.pallas_call(functools.partial(step_kernel, n_col, group), name='step',...]
    pad x2 -> x0, local copies, waits for them, and re-layouts: 2.39 us -> none  [the longest x1 1.22 us: body(): src_all, dst_all = spread(n_row, n_col, jnp.pad(entities, pad))]
    unnamed x5 -> x2, local copies, waits for them, and re-layouts: 3.5 us -> 2.8 us
where the time goes in v1:
time: 113 us
  Pallas kernels  109 us (96%)
  local copies, waits for them, and re-layouts  2.8 us (2%)
    pallas_call x1, Pallas kernels, step_call(): pl.pallas_call(functools.partial(step_kernel, n_col, group), name='step',...  109 us
    unnamed x2, local copies, waits for them, and re-layouts  2.8 us

profile of v1, /device:TPU:0, one launch (start us, length us, event | category | flops | bytes accessed | tf_op | source)
XLA Modules:
  0.0 112.6 jit_solution(506930150021444300)
XLA Ops:
  0.6 109.1 %step.1 = (f32[32,128]{1,0:T(8,128)}, f32[2,32,200]{2,1,0:T(8,128)}) custom-call(s32[4096]{0:T(1024)} %src_i.1, s32[4096]{0:T(1024)} %dst_i.1, s32[4096]{0:T(1024)} %rel_i.1, s32[8]{0:T(128)} %neg_i.1, s32[1,4096]{1,0:T(1,128)} %bitcast.6, bf16[2,200,1024]{2,1,0:T(8,128)(2,1)} %bitcast.4, bf16[2,200,1024]{2,1,0:T(8,128)(2,1)} %bitcast.5), custom_call_target="tpu_custom_call" | custom-call | tf_op jit(solution)/shard_map/step/pallas_call | solution.py:358
  109.8 1.3 %copy.10 = f32[4096]{0:T(1024)} copy(f32[4096]{0:T(1024)} %bitcast.7) | data formatting | bytes 32768
  111.1 1.5 %copy.11 = f32[2,32,200]{2,1,0:T(8,128)} copy(f32[2,32,200]{2,1,0:T(8,128)} %get-tuple-element.9) | data formatting | bytes 102400

commit v2 on v1

--- a/solution.py
+++ b/solution.py
@@ -22,9 +22,9 @@
 
 
 def step_kernel(
-    n_col, group, src_i, dst_i, rel_i, neg_i, rel_row, ent, rel, loss, grad,
-    srcb, dstb, relb, s_tab, o_tab, w_tab, gs, go, gw, qb, pos, key, acc, pairb, tot, inb, zs, zin,
-    loc_sem, send_sem, recv_sem,
+    n_col, group, stages, neg_i, src_row, dst_row, rel_row, ent, rel, loss, grad, late,
+    srcb, dstb, relb, s_tab, o_tab, w_tab, gs, go, gw, qb, dots, key, spot, moved, order_v, order_s, lossp, flag,
+    acc, pairb, tot, inb, zs, zin, loc_sem, send_sem, recv_sem,
 ):
     r, c = lax.axis_index("row"), lax.axis_index("col")
     chip, core = r // 2, r % 2
@@ -140,44 +140,106 @@
                 half = shard * per + p
                 fill_half(srcb, half, (s_tab, half))
 
-    def pick(table, index, g):
+    def pick(table, kind, g, low, rows):
+        top = table.shape[0] - 1
+        keep = (lambda v: v & top) if top & (top + 1) == 0 else (lambda v: jnp.clip(v, 0, top))
+
         def step(i, carry):
-            got = []
-            for u in range(PICKS):
-                got.append(table[index[g * group + i * PICKS + u]])
+            got = [table[keep(order_s[kind, g, low + i * PICKS + u])] for u in range(PICKS)]
             for u in range(PICKS):
                 gs[pl.ds(pl.multiple_of((i * PICKS + u) * 4, 4), 4), :] = got[u]
             return carry
 
-        lax.fori_loop(0, group // PICKS, step, 0)
-
-    def pick_all(table, index, out):
-        def one(g, carry):
-            pick(table, index, g)
-
-            def pack(i, inner):
-                row = pl.multiple_of(i * QROWS, QROWS)
-                at = pl.ds(pl.multiple_of(g * group + row, QROWS), QROWS)
-                for k in range(4):
-                    out[at, k * LANE : (k + 1) * LANE] = gs[pl.ds(row * 4 + k, QROWS, stride=4), :].astype(BF16)
-                return inner
-
-            lax.fori_loop(0, group // QROWS, pack, 0)
-            return carry
-
-        lax.fori_loop(0, groups, one, 0)
-
-    rel_ids = rel_row[...]
+        lax.fori_loop(0, rows // PICKS, step, 0)
+
+    def pick_all(table, kind, out):
+        for low, rows in stages:
+            def one(g, carry, low=low, rows=rows):
+                pick(table, kind, g, low, rows)
+
+                def pack(i, inner):
+                    row = pl.multiple_of(i * QROWS, QROWS)
+                    at = pl.ds(pl.multiple_of(groups * low + g * rows + row, QROWS), QROWS)
+                    for k in range(4):
+                        out[at, k * LANE : (k + 1) * LANE] = gs[pl.ds(row * 4 + k, QROWS, stride=4), :].astype(BF16)
+                    return inner
+
+                lax.fori_loop(0, rows // QROWS, pack, 0)
+                return carry
+
+            lax.fori_loop(0, groups, one, 0)
+
     span = n_rel // (8 * n_col)
+    for g in range(groups):
+        cut = slice(g * group, (g + 1) * group)
+        for kind, ref in enumerate((src_row, dst_row, rel_row)):
+            order_v[kind, g : g + 1, :] = ref[:, cut]
+    halves = lax.div(order_v[0], NEGB)
+    far = jnp.abs(lax.div(halves, per) - c) == n_col - 1
+    last = jnp.logical_and(far, lax.rem(halves, per) == per - 1)
+    early = jnp.where(far, 0.0, 1.0)
+    middle = jnp.where(last, 0.0, 1.0) - early
+    lane_id = lax.broadcasted_iota(jnp.int32, (groups, group), 1).astype(F32)
+    before = lax.broadcasted_iota(jnp.int32, (group, group), 0) < lax.broadcasted_iota(jnp.int32, (group, group), 1)
+    ahead = jnp.dot(
+        jnp.concatenate([early, middle], 0).astype(BF16), jnp.where(before, 1.0, 0.0).astype(BF16),
+        preferred_element_type=F32,
+    )
+    ahead0, ahead1 = ahead[:groups], ahead[groups:]
+    n_early = jnp.sum(early, 1, keepdims=True)
+    n_middle = jnp.sum(middle, 1, keepdims=True)
+    place = jnp.where(
+        far, jnp.where(last, n_early + n_middle + lane_id - ahead0 - ahead1, n_early + ahead1), ahead0
+    )
+    spot[...] = place.astype(jnp.int32)
+    if len(stages) > 1:
+        short = jnp.maximum(
+            jnp.where(n_early < float(stages[1][0]), 1.0, 0.0),
+            jnp.where(n_early + n_middle < float(stages[2][0]), 1.0, 0.0),
+        )
+        lanes = lax.broadcasted_iota(jnp.int32, (1, 2 * WIDE), 1)
+        flag[...] = jnp.where(lanes == WIDE - 1, jnp.sum(short, 0, keepdims=True), 0.0)
+    else:
+        flag[...] = jnp.zeros_like(flag)
+
+    def turn(g):
+        ids = lax.broadcasted_iota(jnp.int32, (group, group), 0)
+        return jnp.where(ids == spot[pl.ds(g, 1), :], 1.0, 0.0).astype(BF16)
+
+    split = []
+    for kind in range(3):
+        split += [lax.div(order_v[kind], LANE), lax.rem(order_v[kind], LANE)]
+    moved[...] = jnp.concatenate(split, 0).astype(F32)
+    pieces = moved[...].astype(BF16)
+    mine = lax.rem(lax.broadcasted_iota(jnp.int32, (6 * groups, group), 0), groups)
+    nt = (((1,), (1,)), ((), ()))
+
+    def reorder(g, carry):
+        got = lax.dot_general(pieces, turn(g), nt, preferred_element_type=F32)
+        moved[...] = jnp.where(mine == g, got, moved[...])
+        return carry
+
+    lax.fori_loop(0, groups, reorder, 0)
+    for kind in range(3):
+        at = kind * 2 * groups
+        order_v[kind] = (moved[at : at + groups] * LANE + moved[at + groups : at + 2 * groups]).astype(jnp.int32)
+    to_scalar = pltpu.make_async_copy(order_v, order_s, loc_sem.at[3])
+    to_scalar.start()
+    rel_ids = order_v[2]
     row_part = lax.div(rel_ids, n_col * span)
-    key[...] = (
+    keys = (
         lax.rem(lax.div(rel_ids, span), n_col) * (8 * span)
         + lax.rem(row_part, 2) * (4 * span) + lax.div(row_part, 2) * span + lax.rem(rel_ids, span)
     )
+    for low, rows in stages:
+        for g in range(groups):
+            at = groups * low + g * rows
+            key[:, at : at + rows] = keys[g : g + 1, low : low + rows]
+    to_scalar.wait()
 
     local_rel.wait()
     fill(lambda p, rows, col: relb[p, rows, pl.ds(col, LANE)], [(w_tab, 0, n_rel)])
-    pick_all(w_tab, rel_i, gw)
+    pick_all(w_tab, 2, gw)
     for move in local_ent:
         move.wait()
     for p in range(per):
@@ -225,78 +287,106 @@
     arrive(M0 + 6, at_dst(md, 0))
     arrive(M0 + 7, at_dst(md, 1))
     fill_dst(md)
-    pick_all(o_tab, dst_i, go)
+    pick_all(o_tab, 1, go)
 
     for way in (1, -1):
         line_wait(way, 1, 1)
         line_send(way, 2, 1)
     fill_src(c - 2)
     fill_src(c + 2)
-    for way in (1, -1):
-        line_wait(way, 2, 0)
-        line_wait(way, 2, 1)
-    fill_src(c - 3)
-    fill_src(c + 3)
-
     eye = lax.broadcasted_iota(jnp.int32, (LANE, LANE), 0) == lax.broadcasted_iota(jnp.int32, (LANE, LANE), 1)
-    nt = (((1,), (1,)), ((), ()))
     cuts = ((0, LANE), (LANE, dim))
 
-    def one_group(g, carry):
-        pick(s_tab, src_i, g)
-
-        def query(i, inner):
-            row = pl.multiple_of(i * QROWS, QROWS)
-            rows = pl.ds(pl.multiple_of(g * group + row, QROWS), QROWS)
-            score = None
+    def main_stage(low_row, size):
+        def one_group(g, carry):
+            pick(s_tab, 0, g, low_row, size)
+            first = groups * low_row + g * size
+
+            def query(i, inner):
+                row = pl.multiple_of(i * QROWS, QROWS)
+                rows = pl.ds(pl.multiple_of(first + row, QROWS), QROWS)
+                score = None
+                for half, (low, high) in enumerate(cuts):
+                    near = lambda p: gs[pl.ds(row * 4 + p * 2 + half, QROWS, stride=4), :]
+                    dense = lambda ref, p: ref[rows, p * WIDE + half * LANE : p * WIDE + (half + 1) * LANE].astype(F32)
+                    sr, si, wr, wi = near(0), near(1), dense(gw, 0), dense(gw, 1)
+                    qr = sr * wr - si * wi
+                    qi = sr * wi + si * wr
+                    add = qr * dense(go, 0) + qi * dense(go, 1)
+                    score = add if score is None else score + add
+                    qb[0, pl.ds(row, QROWS), low:high] = qr[:, : high - low].astype(BF16)
+                    qb[1, pl.ds(row, QROWS), low:high] = qi[:, : high - low].astype(BF16)
+                dots[pl.ds(row, QROWS), :] = score
+                return inner
+
+            lax.fori_loop(0, size // QROWS, query, 0)
+            b = neg_i[g]
+            near = lambda p: dstb[b, p]
+            score = jnp.dot(qb[0, :size], near(0), preferred_element_type=F32)
+            score = score + jnp.dot(qb[1, :size], near(1), preferred_element_type=F32)
+            small = jnp.exp(-jnp.abs(score))
+            soft = jnp.maximum(score, 0.0) + log1p_small(small)
+            ratio = 1.0 / (1.0 + small)
+            weight = jnp.where(score >= 0.0, ratio, small * ratio).astype(BF16)
+            p = jnp.sum(dots[:size], 1, keepdims=True)
+            p_small = jnp.exp(-jnp.abs(p))
+            value = jnp.maximum(-p, 0.0) + log1p_small(p_small) + jnp.sum(soft, 1, keepdims=True) * (1.0 / NEGB)
+            pull = jnp.where(p >= 0.0, p_small, 1.0) / (1.0 + p_small)
+            for i in range(size // LANE):
+                piece = value[i * LANE : (i + 1) * LANE]
+                lossp[pl.ds((low_row // LANE + i) * groups + g, 1), :] = jnp.sum(jnp.where(eye, piece, 0.0), 0, keepdims=True)
+            g_re = lax.dot_general(weight, near(0), nt, preferred_element_type=F32) * (1.0 / NEGB)
+            g_im = lax.dot_general(weight, near(1), nt, preferred_element_type=F32) * (1.0 / NEGB)
+            rows = pl.ds(pl.multiple_of(first, size), size)
             for half, (low, high) in enumerate(cuts):
-                near = lambda p: gs[pl.ds(row * 4 + p * 2 + half, QROWS, stride=4), :]
-                dense = lambda ref, p: ref[rows, p * WIDE + half * LANE : p * WIDE + (half + 1) * LANE].astype(F32)
-                sr, si, wr, wi = near(0), near(1), dense(gw, 0), dense(gw, 1)
-                qr = sr * wr - si * wi
-                qi = sr * wi + si * wr
-                add = qr * dense(go, 0) + qi * dense(go, 1)
-                score = add if score is None else score + add
-                qb[0, pl.ds(row, QROWS), low:high] = qr[:, : high - low].astype(BF16)
-                qb[1, pl.ds(row, QROWS), low:high] = qi[:, : high - low].astype(BF16)
-            pos[pl.ds(row, QROWS), :] = jnp.sum(score, 1, keepdims=True)
-            return inner
-
-        lax.fori_loop(0, group // QROWS, query, 0)
-
-        b = neg_i[g]
-        near = lambda p: dstb[b, p]
-        score = jnp.dot(qb[0], near(0), preferred_element_type=F32)
-        score = score + jnp.dot(qb[1], near(1), preferred_element_type=F32)
-        small = jnp.exp(-jnp.abs(score))
-        soft = jnp.maximum(score, 0.0) + log1p_small(small)
-        turn = 1.0 / (1.0 + small)
-        weight = jnp.where(score >= 0.0, turn, small * turn).astype(BF16)
-        p = pos[...]
-        p_small = jnp.exp(-jnp.abs(p))
-        value = jnp.maximum(-p, 0.0) + log1p_small(p_small) + jnp.sum(soft, 1, keepdims=True) * (1.0 / NEGB)
-        pull = jnp.where(p >= 0.0, p_small, 1.0) / (1.0 + p_small)
-        for i in range(group // LANE):
-            piece = value[i * LANE : (i + 1) * LANE]
-            loss[pl.ds(g * (group // LANE) + i, 1), :] = jnp.sum(jnp.where(eye, piece, 0.0), 0, keepdims=True)
-        g_re = lax.dot_general(weight, near(0), nt, preferred_element_type=F32) * (1.0 / NEGB)
-        g_im = lax.dot_general(weight, near(1), nt, preferred_element_type=F32) * (1.0 / NEGB)
-        rows = pl.ds(pl.multiple_of(g * group, group), group)
-        for half, (low, high) in enumerate(cuts):
-            wide = high - low
-            part = lambda q: gs[pl.ds(q * 2 + half, group, stride=4), :][:, :wide]
-            lanes = lambda q: slice(q * WIDE + low, q * WIDE + high)
-            d_re = g_re[:, low:high] - pull * go[rows, lanes(0)].astype(F32)
-            d_im = g_im[:, low:high] - pull * go[rows, lanes(1)].astype(F32)
-            s_re, s_im = part(0), part(1)
-            gw[rows, lanes(0)] = (d_re * s_re + d_im * s_im).astype(BF16)
-            gw[rows, lanes(1)] = (d_im * s_re - d_re * s_im).astype(BF16)
-        return carry
-
-    lax.fori_loop(0, groups, one_group, 0)
+                wide = high - low
+                part = lambda q: gs[pl.ds(q * 2 + half, size, stride=4), :][:, :wide]
+                lanes = lambda q: slice(q * WIDE + low, q * WIDE + high)
+                d_re = g_re[:, low:high] - pull * go[rows, lanes(0)].astype(F32)
+                d_im = g_im[:, low:high] - pull * go[rows, lanes(1)].astype(F32)
+                s_re, s_im = part(0), part(1)
+                gw[rows, lanes(0)] = (d_re * s_re + d_im * s_im).astype(BF16)
+                gw[rows, lanes(1)] = (d_im * s_re - d_re * s_im).astype(BF16)
+            return carry
+
+        lax.fori_loop(0, groups, one_group, 0)
 
     tile = 8 * span
     edges = gw.shape[0]
+
+    def far_half(p):
+        for way in (1, -1):
+            line_wait(way, n_col - 2, p)
+            shard = c - way * (n_col - 1)
+
+            @pl.when(inside(shard))
+            def _():
+                fill_half(srcb, shard * per + p, (s_tab, shard * per + p))
+
+    def terms(plane, low, high):
+        ids = lax.broadcasted_iota(jnp.int32, (tile, high - low), 0) + plane * tile
+        hot = jnp.where(ids == key[:, low:high], 1.0, 0.0).astype(BF16)
+        return jnp.dot(hot, gw[low:high], preferred_element_type=F32)
+
+    if len(stages) > 1:
+        main_stage(*stages[0])
+        far_half(0)
+        main_stage(*stages[1])
+        done = groups * stages[2][0]
+
+        def begin(plane, carry):
+            acc[plane] = (terms(plane, 0, done) + flag[...]).reshape(acc.shape[1:])
+            return carry
+
+        lax.fori_loop(0, n_col, begin, 0)
+        far_half(1)
+        main_stage(*stages[2])
+    else:
+        done = 0
+        far_half(0)
+        far_half(1)
+        main_stage(*stages[0])
+
     home = [2, 1, 3, 0]
     S0 = M0 + 8
     spots = [(xp, (y * 2 + 1 - x)), (yp, ((1 - y) * 2 + x)), (dp, ((1 - y) * 2 + 1 - x))]
@@ -304,7 +394,7 @@
 
     def pair_up(t):
         arrive(S0 + t, pairb.at[t])
-        tot[t] = acc[t, core] + pairb[t]
+        tot[t] = acc[(c + home[t]) % n_col, core] + pairb[t]
         for k in order:
             peer, there = spots[k]
             start(S0 + 4 + t * 3 + k, tot.at[t, there], inb.at[t, k], peer)
@@ -318,10 +408,9 @@
 
     for t in range(n_col):
         plane = (c + home[t]) % n_col
-        ids = lax.broadcasted_iota(jnp.int32, (tile, edges), 0) + plane * tile
-        hot = jnp.where(ids == key[...], 1.0, 0.0).astype(BF16)
-        acc[t] = jnp.dot(hot, gw[...], preferred_element_type=F32).reshape(2, 4, span, 2 * WIDE)
-        start(S0 + t, acc.at[t, 1 - core], pairb.at[t], mate)
+        part = terms(plane, done, edges).reshape(acc.shape[1:])
+        acc[plane] = acc[plane] + part if done else part
+        start(S0 + t, acc.at[plane, 1 - core], pairb.at[t], mate)
         if t:
             pair_up(t - 1)
     pair_up(n_col - 1)
@@ -329,12 +418,30 @@
     for t in range(n_col - 1):
         zs[t] = plane_sum(t)
         start(Z0 + t, zs.at[t], zin.at[t], (r, (c + home[t]) % n_col))
+    full = jnp.concatenate([lossp[i * groups : (i + 1) * groups] for i in range(group // LANE)], 1)
+    high = full.astype(BF16).astype(F32)
+    mid = (full - high).astype(BF16).astype(F32)
+    low = full - high - mid
+    shares = jnp.concatenate([high, mid, low, jnp.zeros_like(low)], 0).astype(BF16)
+    which = lax.broadcasted_iota(jnp.int32, (groups, group), 0)
+
+    def restore(g, carry):
+        got = jnp.dot(shares, turn(g), preferred_element_type=F32)
+        whole = got[:groups] + got[groups : 2 * groups] + got[2 * groups : 3 * groups]
+        return jnp.where(which == g, whole, carry)
+
+    back = lax.fori_loop(0, groups, restore, jnp.zeros((groups, group), F32))
+    for g in range(groups):
+        for i in range(group // LANE):
+            at = g * (group // LANE) + i
+            loss[at : at + 1, :] = back[g : g + 1, i * LANE : (i + 1) * LANE]
     total = plane_sum(n_col - 1)
     for t in range(n_col - 1):
         arrive(Z0 + t, zin.at[t])
         total = total + zin[t]
     grad[0] = total[:, :dim]
     grad[1] = total[:, WIDE : WIDE + dim]
+    late[...] = total[:8, WIDE - LANE : WIDE]
 
     for cond, move in started:
         if cond is None:
@@ -343,27 +450,30 @@
             pl.when(cond)(move.wait_send)
 
 
-def step_call(n_row, n_col, ent, rel, src_index, dst_index, rel_index, neg_block):
+def step_call(n_row, n_col, fast, ent, rel, src_index, dst_index, rel_index, neg_block):
     edges, groups = src_index.shape[0], neg_block.shape[0]
     group = edges // groups
     parts, dim, count = ent.shape
     n_rel = rel.shape[2]
     span = n_rel // (n_row * n_col)
     chips = n_row // 2
+    stages = ((0, 256), (256, 128), (384, 128)) if fast else ((0, group),)
+    flat = lambda a: a.reshape(1, edges)
     smem = pl.BlockSpec(memory_space=pltpu.SMEM)
     vmem = pl.BlockSpec(memory_space=pltpu.VMEM)
     hbm = pl.BlockSpec(memory_space=pltpu.HBM)
     dma = pltpu.SemaphoreType.DMA
     copies = 4 * (n_col - 1) + 14 + 4 + n_col * 3 + n_col - 1
     return pl.pallas_call(
-        functools.partial(step_kernel, n_col, group),
-        name="step",
+        functools.partial(step_kernel, n_col, group, stages),
+        name="step" if fast else "step_late",
         out_shape=(
             jax.ShapeDtypeStruct((edges // LANE, LANE), F32),
             jax.ShapeDtypeStruct((parts, span, dim), F32),
+            jax.ShapeDtypeStruct((8, LANE), F32),
         ),
-        in_specs=[smem, smem, smem, smem, vmem, hbm, hbm],
-        out_specs=(vmem, vmem),
+        in_specs=[smem, vmem, vmem, vmem, hbm, hbm],
+        out_specs=(vmem, vmem, vmem),
         scratch_shapes=[
             pltpu.VMEM((n_col * count // NEGB, parts, dim, NEGB), BF16),
             pltpu.VMEM((n_row * count // NEGB, parts, dim, NEGB), BF16),
@@ -375,20 +485,26 @@
             pltpu.VMEM((edges, 2 * WIDE), BF16),
             pltpu.VMEM((edges, 2 * WIDE), BF16),
             pltpu.VMEM((parts, group, dim), BF16),
-            pltpu.VMEM((group, 1), F32),
+            pltpu.VMEM((group, LANE), F32),
             pltpu.VMEM((1, edges), jnp.int32),
+            pltpu.VMEM((groups, group), jnp.int32),
+            pltpu.VMEM((6 * groups, group), F32),
+            pltpu.VMEM((3, groups, group), jnp.int32),
+            pltpu.SMEM((3, groups, group), jnp.int32),
+            pltpu.VMEM((edges // LANE, LANE), F32),
+            pltpu.VMEM((1, 2 * WIDE), F32),
             pltpu.VMEM((n_col, 2, chips, span, 2 * WIDE), F32),
             pltpu.VMEM((n_col, chips, span, 2 * WIDE), F32),
             pltpu.VMEM((n_col, chips, span, 2 * WIDE), F32),
             pltpu.VMEM((n_col, 3, span, 2 * WIDE), F32),
             pltpu.VMEM((n_col - 1, span, 2 * WIDE), F32),
             pltpu.VMEM((n_col - 1, span, 2 * WIDE), F32),
-            dma((3,)), dma((copies,)), dma((copies,)),
+            dma((4,)), dma((copies,)), dma((copies,)),
         ],
         compiler_params=pltpu.CompilerParams(
-            collective_id=0, has_side_effects=True, vmem_limit_bytes=67043328
+            collective_id=0 if fast else 1, has_side_effects=True, vmem_limit_bytes=67043328
         ),
-    )(src_index, dst_index, rel_index, neg_block, rel_index.reshape(1, edges), ent, rel)
+    )(neg_block, flat(src_index), flat(dst_index), flat(rel_index), ent, rel)
 
 
 def body(n_row, n_col, entities, relations, src_index, dst_index, rel_index, neg_block):
@@ -398,9 +514,15 @@
     fits = LANE < dim < WIDE and (n_row + n_col) * count * 4 * LANE * 4 <= 26 * 2**20
     if n_row != 8 or n_col != 4 or count != 2 * NEGB or not fits:
         return wide_body(*args)
+    if src_index.shape[0] != 8 * neg_block.shape[0] * 64 or neg_block.shape[0] != 8:
+        return wide_body(*args)
     flip = lambda a: jnp.transpose(a, (0, 2, 1))
-    edge_loss, grad = step_call(
-        n_row, n_col, flip(entities), flip(relations), src_index, dst_index, rel_index, neg_block
+    whole = (flip(entities), flip(relations), src_index, dst_index, rel_index, neg_block)
+    edge_loss, grad, late = step_call(n_row, n_col, True, *whole)
+    edge_loss, grad = lax.cond(
+        late[0, LANE - 1] > 0.0,
+        lambda: tuple(step_call(n_row, n_col, False, *whole)[:2]),
+        lambda: (edge_loss, grad),
     )
     return edge_loss.reshape(-1), grad
 

time: 113 us -> 115 us (1.018)
  local copies, waits for them, and re-layouts: 2.8 us -> 4.05 us
    slice x0 -> x1, local copies, waits for them, and re-layouts: none -> 1.25 us  [body(): late[0, LANE - 1] > 0.0]
where the time goes in v2:
time: 115 us
  Pallas kernels  109 us (95%)
  local copies, waits for them, and re-layouts  4.05 us (4%)
  between operations  1.3 us (1%)
    pallas_call x1, Pallas kernels, step_call(): pl.pallas_call(functools.partial(step_kernel, n_col, group, stages), name...  109 us
    unnamed x2, local copies, waits for them, and re-layouts  2.8 us

profile of v2, /device:TPU:0, one launch (start us, length us, event | category | flops | bytes accessed | tf_op | source)
XLA Modules:
  0.0 114.9 jit_solution(2282620348840565094)
XLA Ops:
  0.6 109.3 %step.1 = (f32[32,128]{1,0:T(8,128)}, f32[2,32,200]{2,1,0:T(8,128)}, f32[8,128]{1,0:T(8,128)}) custom-call(s32[8]{0:T(128)} %neg_i.1, s32[1,4096]{1,0:T(1,128)} %bitcast.14, s32[1,4096]{1,0:T(1,128)} %bitcast.16, s32[1,4096]{1,0:T(1,128)} %bitcast.18, bf16[2,200,1024]{2,1,0:T(8,128)(2,1)} %bitcast.10, bf16[2,200,1024]{2,1,0:T(8,128)(2,1)} %bitcast.12), custom_call_target="tpu_custom_call" | custom-call | tf_op jit(solution)/shard_map/step/pallas_call | solution.py:467
  110.0 1.3 %slice.3 = f32[1,1]{1,0:T(1,128)} slice(f32[8,128]{1,0:T(8,128)} %get-tuple-element.36), slice={[0:1], [127:128]} | slice | bytes 8 | tf_op jit(solution)/shard_map/slice | solution.py:523
  111.9 0.2 conditional.1
  112.1 1.3 %copy.14 = f32[4096]{0:T(1024)} copy(f32[4096]{0:T(1024)} %bitcast.20) | data formatting | bytes 32768
  113.4 1.5 %copy.15 = f32[2,32,200]{2,1,0:T(8,128)} copy(f32[2,32,200]{2,1,0:T(8,128)} %get-tuple-element.53) | data formatting | bytes 102400

commit v3 on v2

--- a/solution.py
+++ b/solution.py
@@ -23,7 +23,7 @@
 
 def step_kernel(
     n_col, group, stages, neg_i, src_row, dst_row, rel_row, ent, rel, loss, grad, late,
-    srcb, dstb, relb, s_tab, o_tab, w_tab, gs, go, gw, qb, dots, key, spot, moved, order_v, order_s, lossp, flag,
+    srcb, dstb, relb, s_tab, o_tab, w_tab, gs, go, gw, qb, dots, key, spot, moved, order_v, order_t, order_s, lossp, flag,
     acc, pairb, tot, inb, zs, zin, loc_sem, send_sem, recv_sem,
 ):
     r, c = lax.axis_index("row"), lax.axis_index("col")
@@ -36,6 +36,7 @@
     dim, count = ent.shape[1], ent.shape[2]
     n_rel = rel.shape[2]
     groups = neg_i.shape[0]
+    edges = gw.shape[0]
     per = count // NEGB
     rest = dim - LANE
 
@@ -143,14 +144,17 @@
     def pick(table, kind, g, low, rows):
         top = table.shape[0] - 1
         keep = (lambda v: v & top) if top & (top + 1) == 0 else (lambda v: jnp.clip(v, 0, top))
+        start_row = kind * (edges // LANE) + low // LANE * groups + g
 
         def step(i, carry):
-            got = [table[keep(order_s[kind, g, low + i * PICKS + u])] for u in range(PICKS)]
-            for u in range(PICKS):
-                gs[pl.ds(pl.multiple_of((i * PICKS + u) * 4, 4), 4), :] = got[u]
+            row = start_row + i * groups
+            for part in range(0, LANE, PICKS):
+                got = [table[keep(order_s[row, part + u])] for u in range(PICKS)]
+                for u in range(PICKS):
+                    gs[pl.ds(pl.multiple_of((i * LANE + part + u) * 4, 4), 4), :] = got[u]
             return carry
 
-        lax.fori_loop(0, rows // PICKS, step, 0)
+        lax.fori_loop(0, rows // LANE, step, 0)
 
     def pick_all(table, kind, out):
         for low, rows in stages:
@@ -223,7 +227,12 @@
     for kind in range(3):
         at = kind * 2 * groups
         order_v[kind] = (moved[at : at + groups] * LANE + moved[at + groups : at + 2 * groups]).astype(jnp.int32)
-    to_scalar = pltpu.make_async_copy(order_v, order_s, loc_sem.at[3])
+    blocks = group // LANE
+    for kind in range(3):
+        for i in range(blocks):
+            at = (kind * blocks + i) * groups
+            order_t[at : at + groups, :] = order_v[kind, :, i * LANE : (i + 1) * LANE]
+    to_scalar = pltpu.make_async_copy(order_t, order_s, loc_sem.at[3])
     to_scalar.start()
     rel_ids = order_v[2]
     row_part = lax.div(rel_ids, n_col * span)
@@ -352,7 +361,6 @@
         lax.fori_loop(0, groups, one_group, 0)
 
     tile = 8 * span
-    edges = gw.shape[0]
 
     def far_half(p):
         for way in (1, -1):
@@ -490,7 +498,8 @@
             pltpu.VMEM((groups, group), jnp.int32),
             pltpu.VMEM((6 * groups, group), F32),
             pltpu.VMEM((3, groups, group), jnp.int32),
-            pltpu.SMEM((3, groups, group), jnp.int32),
+            pltpu.VMEM((3 * edges // LANE, LANE), jnp.int32),
+            pltpu.SMEM((3 * edges // LANE, LANE), jnp.int32),
             pltpu.VMEM((edges // LANE, LANE), F32),
             pltpu.VMEM((1, 2 * WIDE), F32),
             pltpu.VMEM((n_col, 2, chips, span, 2 * WIDE), F32),

time: 115 us -> 96.7 us (0.84)
  Pallas kernels: 109 us -> 90.8 us
    pallas_call x1, Pallas kernels: 109 us -> 90.8 us  [step_call(): pl.pallas_call(functools.partial(step_kernel, n_col, group, stages), name...]
where the time goes in v3:
time: 96.7 us; the launch traced here: 96.3 us
  Pallas kernels  90.8 us (94%)
  local copies, waits for them, and re-layouts  4.05 us (4%)
  between operations  1.3 us (1%)
    pallas_call x1, Pallas kernels, step_call(): pl.pallas_call(functools.partial(step_kernel, n_col, group, stages), name...  90.8 us
    unnamed x2, local copies, waits for them, and re-layouts  2.8 us

profile of v3, /device:TPU:0, one launch (start us, length us, event | category | flops | bytes accessed | tf_op | source)
XLA Modules:
  0.0 96.3 jit_solution(6845588106749966348)
XLA Ops:
  0.6 90.8 %step.1 = (f32[32,128]{1,0:T(8,128)}, f32[2,32,200]{2,1,0:T(8,128)}, f32[8,128]{1,0:T(8,128)}) custom-call(s32[8]{0:T(128)} %neg_i.1, s32[1,4096]{1,0:T(1,128)} %bitcast.14, s32[1,4096]{1,0:T(1,128)} %bitcast.16, s32[1,4096]{1,0:T(1,128)} %bitcast.18, bf16[2,200,1024]{2,1,0:T(8,128)(2,1)} %bitcast.10, bf16[2,200,1024]{2,1,0:T(8,128)(2,1)} %bitcast.12), custom_call_target="tpu_custom_call" | custom-call | tf_op jit(solution)/shard_map/step/pallas_call | solution.py:475
  91.4 1.3 %slice.3 = f32[1,1]{1,0:T(1,128)} slice(f32[8,128]{1,0:T(8,128)} %get-tuple-element.36), slice={[0:1], [127:128]} | slice | bytes 8 | tf_op jit(solution)/shard_map/slice | solution.py:532
  93.3 0.2 conditional.1
  93.5 1.3 %copy.14 = f32[4096]{0:T(1024)} copy(f32[4096]{0:T(1024)} %bitcast.20) | data formatting | bytes 32768
  94.9 1.5 %copy.15 = f32[2,32,200]{2,1,0:T(8,128)} copy(f32[2,32,200]{2,1,0:T(8,128)} %get-tuple-element.53) | data formatting | bytes 102400

commit v4 on v3

--- a/solution.py
+++ b/solution.py
@@ -14,7 +14,8 @@
 F32 = jnp.float32
 BF16 = jnp.bfloat16
 PICKS = 32
-QROWS = 32
+QROWS = 64
+PROWS = 128
 
 
 def log1p_small(u):
@@ -109,19 +110,20 @@
 
     def fill(read, targets):
         def step(j, carry):
-            col = pl.multiple_of(j * LANE, LANE)
-            for part in range(2):
-                low = read(part, slice(0, LANE), col).astype(F32).T
-                high = read(part, slice(LANE, dim), col).astype(F32)
-                high = jnp.concatenate([high, jnp.zeros((LANE - rest, LANE), F32)], 0).T
-                for table, first, _ in targets:
-                    flat = table.reshape(table.shape[0] * 4, LANE)
-                    at = first + col * 4 + part * 2
-                    flat[pl.ds(at, LANE, stride=4), :] = low
-                    flat[pl.ds(at + 1, LANE, stride=4), :] = high
+            for both in range(2):
+                col = pl.multiple_of(j * (2 * LANE) + both * LANE, LANE)
+                for part in range(2):
+                    low = read(part, slice(0, LANE), col).astype(F32).T
+                    high = read(part, slice(LANE, dim), col).astype(F32)
+                    high = jnp.concatenate([high, jnp.zeros((LANE - rest, LANE), F32)], 0).T
+                    for table, first, _ in targets:
+                        flat = table.reshape(table.shape[0] * 4, LANE)
+                        at = first + col * 4 + part * 2
+                        flat[pl.ds(at, LANE, stride=4), :] = low
+                        flat[pl.ds(at + 1, LANE, stride=4), :] = high
             return carry
 
-        lax.fori_loop(0, targets[0][2] // LANE, step, 0)
+        lax.fori_loop(0, targets[0][2] // (2 * LANE), step, 0)
 
     def fill_half(buf, half, *tables):
         fill(
@@ -162,13 +164,13 @@
                 pick(table, kind, g, low, rows)
 
                 def pack(i, inner):
-                    row = pl.multiple_of(i * QROWS, QROWS)
-                    at = pl.ds(pl.multiple_of(groups * low + g * rows + row, QROWS), QROWS)
+                    row = pl.multiple_of(i * PROWS, PROWS)
+                    at = pl.ds(pl.multiple_of(groups * low + g * rows + row, PROWS), PROWS)
                     for k in range(4):
-                        out[at, k * LANE : (k + 1) * LANE] = gs[pl.ds(row * 4 + k, QROWS, stride=4), :].astype(BF16)
+                        out[at, k * LANE : (k + 1) * LANE] = gs[pl.ds(row * 4 + k, PROWS, stride=4), :].astype(BF16)
                     return inner
 
-                lax.fori_loop(0, rows // QROWS, pack, 0)
+                lax.fori_loop(0, rows // PROWS, pack, 0)
                 return carry
 
             lax.fori_loop(0, groups, one, 0)
@@ -533,7 +535,22 @@
         lambda: tuple(step_call(n_row, n_col, False, *whole)[:2]),
         lambda: (edge_loss, grad),
     )
+    edge_loss, grad = settle(edge_loss, grad)
     return edge_loss.reshape(-1), grad
+
+
+def settle_kernel(loss_in, grad_in, loss, grad):
+    loss[...] = loss_in[...]
+    grad[...] = grad_in[...]
+
+
+def settle(edge_loss, grad):
+    shape = lambda a: jax.ShapeDtypeStruct(a.shape, a.dtype)
+    vmem = pl.BlockSpec(memory_space=pltpu.VMEM)
+    return pl.pallas_call(
+        settle_kernel, name="settle", out_shape=(shape(edge_loss), shape(grad)),
+        in_specs=[vmem, vmem], out_specs=(vmem, vmem),
+    )(edge_loss, grad)
 
 
 def bucket_terms(picked_src, picked_dst, negatives, relations, rel_ids):

time: 96.7 us -> 93.8 us (0.970)
  local copies, waits for them, and re-layouts: 4.05 us -> 1.26 us
    unnamed x2 -> x0, local copies, waits for them, and re-layouts: 2.8 us -> none
    pallas_call x1, Pallas kernels: 90.8 us -> 89.1 us  [step_call(): pl.pallas_call(functools.partial(step_kernel, n_col, group, stages), name...]
    pallas_call x0 -> x1, Pallas kernels: none -> 1.5 us  [settle(): pl.pallas_call(settle_kernel, name='settle', out_shape=(shape(edge_loss),...]
where the time goes in v4:
time: 93.8 us; the launch traced here: 93.4 us
  Pallas kernels  90.6 us (97%)
  between operations  1.3 us (1%)
  local copies, waits for them, and re-layouts  1.26 us (1%)
    pallas_call x1, Pallas kernels, step_call(): pl.pallas_call(functools.partial(step_kernel, n_col, group, stages), name...  89.1 us

profile of v4, /device:TPU:0, one launch (start us, length us, event | category | flops | bytes accessed | tf_op | source)
XLA Modules:
  0.0 93.4 jit_solution(18018140229034987982)
XLA Ops:
  0.6 89.1 %step.1 = (f32[32,128]{1,0:T(8,128)}, f32[2,32,200]{2,1,0:T(8,128)}, f32[8,128]{1,0:T(8,128)}) custom-call(s32[8]{0:T(128)} %neg_i.1, s32[1,4096]{1,0:T(1,128)} %bitcast.14, s32[1,4096]{1,0:T(1,128)} %bitcast.16, s32[1,4096]{1,0:T(1,128)} %bitcast.18, bf16[2,200,1024]{2,1,0:T(8,128)(2,1)} %bitcast.10, bf16[2,200,1024]{2,1,0:T(8,128)(2,1)} %bitcast.12), custom_call_target="tpu_custom_call" | custom-call | tf_op jit(solution)/shard_map/step/pallas_call | solution.py:477
  89.8 1.3 %slice.3 = f32[1,1]{1,0:T(1,128)} slice(f32[8,128]{1,0:T(8,128)} %get-tuple-element.33), slice={[0:1], [127:128]} | slice | bytes 8 | tf_op jit(solution)/shard_map/slice | solution.py:534
  91.7 0.2 conditional.1
  91.9 1.5 %settle.1 = (f32[32,128]{1,0:T(8,128)}, f32[2,32,200]{2,1,0:T(8,128)}) custom-call(f32[32,128]{1,0:T(8,128)} %get-tuple-element.36.loss_in, f32[2,32,200]{2,1,0:T(8,128)} %get-tuple-element.37.grad_in), custom_call_target="tpu_custom_call" | custom-call | tf_op jit(solution)/shard_map/settle/pallas_call | solution.py:550

commit v5 on v4

--- a/solution.py
+++ b/solution.py
@@ -14,7 +14,7 @@
 F32 = jnp.float32
 BF16 = jnp.bfloat16
 PICKS = 32
-QROWS = 64
+QROWS = 128
 PROWS = 128
 
 
@@ -110,8 +110,8 @@
 
     def fill(read, targets):
         def step(j, carry):
-            for both in range(2):
-                col = pl.multiple_of(j * (2 * LANE) + both * LANE, LANE)
+            for both in range(4):
+                col = pl.multiple_of(j * (4 * LANE) + both * LANE, LANE)
                 for part in range(2):
                     low = read(part, slice(0, LANE), col).astype(F32).T
                     high = read(part, slice(LANE, dim), col).astype(F32)
@@ -123,7 +123,7 @@
                         flat[pl.ds(at + 1, LANE, stride=4), :] = high
             return carry
 
-        lax.fori_loop(0, targets[0][2] // (2 * LANE), step, 0)
+        lax.fori_loop(0, targets[0][2] // (4 * LANE), step, 0)
 
     def fill_half(buf, half, *tables):
         fill(

time: 93.8 us -> 92 us (0.981)
  Pallas kernels: 90.6 us -> 88.8 us
    pallas_call x1, Pallas kernels: 89.1 us -> 87.4 us  [step_call(): pl.pallas_call(functools.partial(step_kernel, n_col, group, stages), name...]
where the time goes in v5:
time: 92 us; the launch traced here: 91.6 us
  Pallas kernels  88.8 us (97%)
  between operations  1.3 us (1%)
  local copies, waits for them, and re-layouts  1.26 us (1%)
    pallas_call x1, Pallas kernels, step_call(): pl.pallas_call(functools.partial(step_kernel, n_col, group, stages), name...  87.4 us

profile of v5, /device:TPU:0, one launch (start us, length us, event | category | flops | bytes accessed | tf_op | source)
XLA Modules:
  0.0 91.6 jit_solution(6201922235487447677)
XLA Ops:
  0.6 87.4 %step.1 = (f32[32,128]{1,0:T(8,128)}, f32[2,32,200]{2,1,0:T(8,128)}, f32[8,128]{1,0:T(8,128)}) custom-call(s32[8]{0:T(128)} %neg_i.1, s32[1,4096]{1,0:T(1,128)} %bitcast.14, s32[1,4096]{1,0:T(1,128)} %bitcast.16, s32[1,4096]{1,0:T(1,128)} %bitcast.18, bf16[2,200,1024]{2,1,0:T(8,128)(2,1)} %bitcast.10, bf16[2,200,1024]{2,1,0:T(8,128)(2,1)} %bitcast.12), custom_call_target="tpu_custom_call" | custom-call | tf_op jit(solution)/shard_map/step/pallas_call | solution.py:477
  88.0 1.3 %slice.3 = f32[1,1]{1,0:T(1,128)} slice(f32[8,128]{1,0:T(8,128)} %get-tuple-element.33), slice={[0:1], [127:128]} | slice | bytes 8 | tf_op jit(solution)/shard_map/slice | solution.py:534
  89.9 0.2 conditional.1
  90.1 1.5 %settle.1 = (f32[32,128]{1,0:T(8,128)}, f32[2,32,200]{2,1,0:T(8,128)}) custom-call(f32[32,128]{1,0:T(8,128)} %get-tuple-element.36.loss_in, f32[2,32,200]{2,1,0:T(8,128)} %get-tuple-element.37.grad_in), custom_call_target="tpu_custom_call" | custom-call | tf_op jit(solution)/shard_map/settle/pallas_call | solution.py:550
